TPU v7x, 32 devices: a whole 2x2x4 slice. The times are simulated.
32 devices in a mesh: groups: 2 (over x), bay: 16 (over z, y, core).
Axes of the slice: x: 2, y: 2, z: 4, core: 2. Of those that a mesh axis runs over, the one named last changes fastest.
Arguments:
- traces: bfloat16 [16, 512, 2048], P('bay', 'groups'), parts along dimension 1, may hold values from -6 to 6
- operator: bfloat16 [16, 2048, 2048], P('bay'), may hold values from -0.09375 to 0.09375
- loads: bfloat16 [16, 16, 2048], P('bay'), may hold values from -6 to 6
- seeds: int32 [512], P('groups'), parts along dimension 0, may hold values from 0 to 99999
- patches: int32 [16, 512], P('bay', 'groups'), parts along dimension 1, may hold values from 0 to 15
- trace_map: int32 [16, 1024], P('bay'), may hold values from 0 to 1023, each once within a row
Outputs:
- final_traces: bfloat16 [16, 512, 2048], P('bay', 'groups'), parts along dimension 1
There are 2 independent parts, one for each index of `groups`. A program takes and returns all parts, laid end to end along the dimension named above; an argument that names none is the same for every part. Nothing has to cross between parts.
Inputs may be any that keep to these rules, and one draw needn't show every extreme that they name: `trace_map`: each row is a permutation of 0 to 1023.
All inputs are finite; a program needn't handle non-finite values.
Results may differ from a plain program's by a relative error of at most 0.0065.
Values may be sent and summed in bfloat16 or wider, within the bound.
A program may use at most 64 MiB of HBM per device.

v0:
```python
import functools

import jax
import jax.numpy as jnp
from jax import lax
from jax.experimental import pallas as pl
from jax.experimental.pallas import tpu as pltpu
from jax.sharding import PartitionSpec as P

TICKS = 6
STRIPS = 4
CHUNKS = 2
PIECES = 4
PERIOD = 97
LANES = 512
MESH = pl.DeviceIdType.MESH


def dot(a, b):
    return jnp.dot(a, b, preferred_element_type=jnp.float32)


def kernel(
    count, traces, operator, loads, seeds, patches, trace_map, out,
    weights, mapped, one_hot, state_on, state_near, state_far, got_on, got_near, got_far,
    total, table, seed_row, pick_row, map_row, picked,
    in_sem, weight_sem, trace_sem, send_sem, recv_sem,
):
    me = lax.axis_index("bay")
    rows, size = state_on.shape[2:]
    lateral = state_near.shape[2]
    onward = PIECES * size
    width = onward + 2 * lateral
    part = rows // CHUNKS
    has_next = me + STRIPS < count
    has_prev = me >= STRIPS
    near = me + 1 - 2 * (me % 2)
    far = me + 2 - 4 * ((me // 2) % 2)
    targets = (me + STRIPS,) * PIECES + (near, far)
    starts = tuple(q * size for q in range(PIECES)) + (onward, onward + lateral)
    sizes = (size,) * PIECES + (lateral, lateral)
    sides = (PIECES, PIECES + 1)

    def rows_of(c):
        return pl.ds(c * part, part)

    def held(t, c, k):
        if k < PIECES:
            return state_on.at[t, k, rows_of(c)]
        return (state_near, state_far)[k - PIECES].at[t, rows_of(c)]

    def got(t, c, k):
        if k < PIECES:
            return got_on.at[t, k, rows_of(c)]
        return (got_near, got_far)[k - PIECES].at[t, rows_of(c)]

    small = [
        pltpu.make_async_copy(src, dst, in_sem.at[i])
        for i, (src, dst) in enumerate(
            ((trace_map, map_row), (seeds, seed_row), (patches, pick_row), (loads.at[0], table))
        )
    ]
    first = [
        [
            pltpu.make_async_copy(
                traces.at[0, rows_of(c), pl.ds(starts[k], sizes[k])], held(0, c, k), trace_sem.at[c, k]
            )
            for k in range(PIECES + 2)
        ]
        for c in range(CHUNKS)
    ]
    halves = [
        pltpu.make_async_copy(
            operator.at[0, pl.ds(h * onward, onward)], weights.at[pl.ds(h * onward, onward)], weight_sem.at[h]
        )
        for h in range(2)
    ]
    for copy in first[0]:
        copy.start()

    barrier = pltpu.get_barrier_semaphore()

    def greet(device):
        pl.semaphore_signal(barrier, inc=1, device_id={"bay": device}, device_id_type=MESH)

    greet(near)
    greet(far)

    @pl.when(has_next)
    def _():
        greet(me + STRIPS)

    @pl.when(has_prev)
    def _():
        greet(me - STRIPS)

    for copy in small:
        copy.start()
    for c in range(1, CHUNKS):
        for copy in first[c]:
            copy.start()

    pl.semaphore_wait(barrier, 2 + has_next.astype(jnp.int32) + has_prev.astype(jnp.int32))

    def remote(t, c, k):
        return pltpu.make_async_remote_copy(
            src_ref=held(t, c, k),
            dst_ref=got(t, c, k),
            send_sem=send_sem.at[t, c, k],
            recv_sem=recv_sem.at[t, c, k],
            device_id={"bay": targets[k]},
            device_id_type=MESH,
        )

    def send_onward(t, c, pieces):
        @pl.when(has_next)
        def _():
            for k in pieces:
                remote(t, c, k).start()

    for c in range(CHUNKS):
        for k in range(PIECES):
            first[c][k].wait()
            send_onward(0, c, (k,))
        for k in sides:
            first[c][k].wait()
            remote(0, c, k).start()
        if c == 0:
            for copy in halves:
                copy.start()

    @pl.when(jnp.logical_not(has_prev))
    def _():
        got_on[...] = jnp.zeros_like(got_on)

    for copy in small:
        copy.wait()
    place = lax.broadcasted_iota(jnp.int32, one_hot.shape, 0)
    one_hot[...] = jnp.where(place == map_row[...], 1.0, 0.0).astype(jnp.bfloat16)
    value = seed_row[...] * 7
    guess = (value.astype(jnp.float32) * (1.0 / PERIOD)).astype(jnp.int32)
    rest = value - guess * PERIOD
    rest = jnp.where(rest < 0, rest + PERIOD, rest)
    rest = jnp.where(rest >= PERIOD, rest - PERIOD, rest)
    chosen = lax.broadcasted_iota(jnp.int32, picked.shape[1:], 0) == pick_row[...]
    for t in range(TICKS):
        turn = rest + (13 * t) % PERIOD
        turn = jnp.where(turn >= PERIOD, turn - PERIOD, turn)
        amplitude = (turn - 48).astype(jnp.float32) / 32.0
        picked[t] = jnp.where(chosen, amplitude, 0.0).astype(jnp.bfloat16)

    halves[0].wait()

    @pl.loop(0, width // LANES)
    def _(n):
        at = pl.ds(pl.multiple_of(n * LANES, LANES), LANES)
        for m in range(0, onward, 256):
            mapped[m : m + 256, at] = dot(one_hot[m : m + 256, :], weights[:onward, at]).astype(jnp.bfloat16)

    halves[1].wait()

    def sideways(t, c):
        here = rows_of(c)
        for k in sides:
            remote(t, c, k).wait_recv()

        @pl.loop(0, width // LANES)
        def _(n):
            at = pl.ds(pl.multiple_of(n * LANES, LANES), LANES)
            source = lax.dot_general(
                picked[t, :, here], table[:, at], (((0,), (0,)), ((), ())), preferred_element_type=jnp.float32
            )
            total[here, at] = (
                source
                + dot(got_near[t, here], weights[onward : onward + lateral, at])
                + dot(got_far[t, here], weights[onward + lateral :, at])
            )

    def arrive(t, c, pieces):
        @pl.when(has_prev)
        def _():
            for k in pieces:
                remote(t, c, k).wait_recv()

    def block(t, c, column, pieces):
        here = rows_of(c)
        at = pl.ds(column, LANES)
        incoming = jnp.concatenate([got_on[t, q, here] for q in pieces], axis=1)
        return total[here, at] + dot(incoming, mapped[pieces[0] * size : (pieces[-1] + 1) * size, at])

    every = tuple(range(PIECES))

    @pl.loop(0, TICKS - 1)
    def _(t):
        for c in range(CHUNKS):
            here = rows_of(c)
            sideways(t, c)
            arrive(t, c, every)
            for column in range(0, onward, LANES):
                value = block(t, c, column, every).astype(jnp.bfloat16)
                pieces = tuple(range(column // size, (column + LANES) // size))
                for q in pieces:
                    state_on[t + 1, q, here] = value[:, q * size - column : (q + 1) * size - column]
                send_onward(t + 1, c, pieces)
            for k in sides:
                for column in range(0, lateral, LANES):
                    value = block(t, c, starts[k] + column, every).astype(jnp.bfloat16)
                    (state_near, state_far)[k - PIECES][t + 1, here, column : column + LANES] = value
                remote(t + 1, c, k).start()

    columns = range(0, width, LANES)
    last = TICKS - 1
    for c in range(CHUNKS):
        here = rows_of(c)
        sideways(last, c)
        rounds = (every,) if c < CHUNKS - 1 else tuple((q,) for q in every)
        for pieces in rounds[:-1]:
            arrive(last, c, pieces)
            for column in columns:
                total[here, column : column + LANES] = block(last, c, column, pieces)
        arrive(last, c, rounds[-1])
        for column in columns:
            out[0, here, column : column + LANES] = block(last, c, column, rounds[-1]).astype(jnp.bfloat16)

    @pl.loop(0, TICKS)
    def _(t):
        for c in range(CHUNKS):
            for k in sides:
                remote(t, c, k).wait_send()

            @pl.when(has_next)
            def _():
                for k in every:
                    remote(t, c, k).wait_send()


def on_device(count, traces, operator, loads, seeds, patches, trace_map):
    _, rows, width = traces.shape
    onward = trace_map.shape[1]
    lateral = (width - onward) // 2
    depth = loads.shape[1]
    bf16, i32 = jnp.bfloat16, jnp.int32
    anywhere = pl.BlockSpec(memory_space=pl.ANY)
    dma = pltpu.SemaphoreType.DMA
    flows = PIECES + 2
    side = pltpu.VMEM((TICKS, rows, lateral), bf16)
    slots = (pltpu.VMEM((TICKS, PIECES, rows, onward // PIECES), bf16), side, side)
    return pl.pallas_call(
        functools.partial(kernel, count),
        name="sweep",
        out_shape=pltpu.VMEM(traces.shape, bf16),
        in_specs=[anywhere] * 6,
        out_specs=pl.BlockSpec(memory_space=pltpu.VMEM),
        scratch_shapes=[
            pltpu.VMEM((width, width), bf16),
            pltpu.VMEM((onward, width), bf16),
            pltpu.VMEM((onward, onward), bf16),
            *slots,
            *slots,
            pltpu.VMEM((rows, width), jnp.float32),
            pltpu.VMEM((depth, width), bf16),
            pltpu.VMEM((1, rows), i32),
            pltpu.VMEM((1, rows), i32),
            pltpu.VMEM((1, onward), i32),
            pltpu.VMEM((TICKS, depth, rows), bf16),
            dma((4,)),
            dma((2,)),
            dma((CHUNKS, flows)),
            dma((TICKS, CHUNKS, flows)),
            dma((TICKS, CHUNKS, flows)),
        ],
        compiler_params=pltpu.CompilerParams(
            collective_id=0, has_side_effects=True, vmem_limit_bytes=60 * 2**20
        ),
    )(traces, operator, loads, seeds.reshape(1, rows), patches, trace_map)


def solution(mesh):
    placed = (
        P("bay", "groups", None),
        P("bay", None, None),
        P("bay", None, None),
        P("groups"),
        P("bay", "groups"),
        P("bay", None),
    )
    return jax.shard_map(
        functools.partial(on_device, mesh.shape["bay"]),
        mesh=mesh,
        in_specs=placed,
        out_specs=P("bay", "groups", None),
        check_vma=False,
    )
```

profile of v0, /device:TPU:0, one launch (start us, length us, event | category | flops | bytes accessed | tf_op | source)
XLA Modules:
  0.0 72.8 jit_solution(2274351365983411846)
XLA Ops:
  0.0 71.9 %sweep.1 = bf16[1,256,2048]{2,1,0:T(8,128)(2,1)S(1)} custom-call(bf16[1,256,2048]{2,1,0:T(8,128)(2,1)} %traces.1, bf16[1,2048,2048]{2,1,0:T(8,128)(2,1)} %operator.1, bf16[1,16,2048]{2,1,0:T(8,128)(2,1)} %loads.1, s32[1,256]{1,0:T(1,128)} %bitcast.1, s32[1,256]{1,0:T(1,128)} %patches.1, s32[1,1024]{1,0:T(1,128)} %trace_map.1), custom_call_target="tpu_custom_call" | custom-call | tf_op jit(solution)/shard_map/sweep/pallas_call | solution.py:248
  71.9 1.0 %copy.8 = bf16[1,256,2048]{2,1,0:T(8,128)(2,1)} copy(bf16[1,256,2048]{2,1,0:T(8,128)(2,1)S(1)} %sweep.1) | data formatting | bytes 2097152
where the time goes:
time: 73 us; the launch traced here: 72.8 us
  Pallas kernels  71.9 us (98%)
  local copies, waits for them, and re-layouts  0.97 us (1%)
    pallas_call x1, Pallas kernels, on_device(): pl.pallas_call(functools.partial(kernel, count), name='sweep', out_shape=...  71.9 us

commit v1 on v0

--- a/solution.py
+++ b/solution.py
@@ -22,13 +22,13 @@
 
 def kernel(
     count, traces, operator, loads, seeds, patches, trace_map, out,
-    weights, mapped, one_hot, state_on, state_near, state_far, got_on, got_near, got_far,
+    weights, mapped, one_hot, state_on, state_side, got_on, got_side,
     total, table, seed_row, pick_row, map_row, picked,
-    in_sem, weight_sem, trace_sem, send_sem, recv_sem,
+    in_sem, weight_sem, trace_sem, send_sem, on_sem, side_sem,
 ):
     me = lax.axis_index("bay")
     rows, size = state_on.shape[2:]
-    lateral = state_near.shape[2]
+    lateral = state_side.shape[3]
     onward = PIECES * size
     width = onward + 2 * lateral
     part = rows // CHUNKS
@@ -47,12 +47,12 @@
     def held(t, c, k):
         if k < PIECES:
             return state_on.at[t, k, rows_of(c)]
-        return (state_near, state_far)[k - PIECES].at[t, rows_of(c)]
+        return state_side.at[t, k - PIECES, rows_of(c)]
 
     def got(t, c, k):
         if k < PIECES:
             return got_on.at[t, k, rows_of(c)]
-        return (got_near, got_far)[k - PIECES].at[t, rows_of(c)]
+        return got_side.at[t, k - PIECES, rows_of(c)]
 
     small = [
         pltpu.make_async_copy(src, dst, in_sem.at[i])
@@ -63,7 +63,7 @@
     first = [
         [
             pltpu.make_async_copy(
-                traces.at[0, rows_of(c), pl.ds(starts[k], sizes[k])], held(0, c, k), trace_sem.at[c, k]
+                traces.at[0, rows_of(c), pl.ds(starts[k], sizes[k])], held(0, c, k), trace_sem.at[c, k // PIECES]
             )
             for k in range(PIECES + 2)
         ]
@@ -86,10 +86,6 @@
     greet(near)
     greet(far)
 
-    @pl.when(has_next)
-    def _():
-        greet(me + STRIPS)
-
     @pl.when(has_prev)
     def _():
         greet(me - STRIPS)
@@ -100,17 +96,36 @@
         for copy in first[c]:
             copy.start()
 
-    pl.semaphore_wait(barrier, 2 + has_next.astype(jnp.int32) + has_prev.astype(jnp.int32))
-
-    def remote(t, c, k):
+    pl.semaphore_wait(barrier, 2 + has_next.astype(jnp.int32))
+
+    last = TICKS - 1
+
+    def signal_of(t, c, k):
+        if k >= PIECES:
+            return side_sem.at[t % 2, c]
+        alone = k * ((t + 1) // TICKS) if c == CHUNKS - 1 else 0
+        return on_sem.at[t * CHUNKS + c + alone]
+
+    def copy_to(device, src, dst, kind, signal):
         return pltpu.make_async_remote_copy(
-            src_ref=held(t, c, k),
-            dst_ref=got(t, c, k),
-            send_sem=send_sem.at[t, c, k],
-            recv_sem=recv_sem.at[t, c, k],
-            device_id={"bay": targets[k]},
+            src_ref=src,
+            dst_ref=dst,
+            send_sem=send_sem.at[kind],
+            recv_sem=signal,
+            device_id={"bay": device},
             device_id_type=MESH,
         )
+
+    def remote(t, c, k):
+        return copy_to(targets[k], held(t, c, k), got(t, c, k), k // PIECES, signal_of(t, c, k))
+
+    def all_onward(t, c):
+        here = (t, slice(None), rows_of(c))
+        return copy_to(targets[0], state_on.at[here], got_on.at[here], 0, signal_of(t, c, 0))
+
+    def both_sides(t, c):
+        here = (t, slice(None), rows_of(c))
+        return copy_to(near, state_side.at[here], got_side.at[here], 1, signal_of(t, c, PIECES))
 
     def send_onward(t, c, pieces):
         @pl.when(has_next)
@@ -118,12 +133,16 @@
             for k in pieces:
                 remote(t, c, k).start()
 
+    def loaded(c, buffer, kind):
+        dst = buffer.at[0, :, rows_of(c)]
+        pltpu.make_async_copy(dst, dst, trace_sem.at[c, kind]).wait()
+
+    every = tuple(range(PIECES))
     for c in range(CHUNKS):
-        for k in range(PIECES):
-            first[c][k].wait()
-            send_onward(0, c, (k,))
+        loaded(c, state_on, 0)
+        send_onward(0, c, every)
+        loaded(c, state_side, 1)
         for k in sides:
-            first[c][k].wait()
             remote(0, c, k).start()
         if c == 0:
             for copy in halves:
@@ -161,8 +180,7 @@
 
     def sideways(t, c):
         here = rows_of(c)
-        for k in sides:
-            remote(t, c, k).wait_recv()
+        both_sides(t, c).wait_recv()
 
         @pl.loop(0, width // LANES)
         def _(n):
@@ -172,23 +190,24 @@
             )
             total[here, at] = (
                 source
-                + dot(got_near[t, here], weights[onward : onward + lateral, at])
-                + dot(got_far[t, here], weights[onward + lateral :, at])
+                + dot(got_side[t, 0, here], weights[onward : onward + lateral, at])
+                + dot(got_side[t, 1, here], weights[onward + lateral :, at])
             )
 
     def arrive(t, c, pieces):
         @pl.when(has_prev)
         def _():
-            for k in pieces:
-                remote(t, c, k).wait_recv()
+            if pieces == every:
+                all_onward(t, c).wait_recv()
+            else:
+                for k in pieces:
+                    remote(t, c, k).wait_recv()
 
     def block(t, c, column, pieces):
         here = rows_of(c)
         at = pl.ds(column, LANES)
         incoming = jnp.concatenate([got_on[t, q, here] for q in pieces], axis=1)
         return total[here, at] + dot(incoming, mapped[pieces[0] * size : (pieces[-1] + 1) * size, at])
-
-    every = tuple(range(PIECES))
 
     @pl.loop(0, TICKS - 1)
     def _(t):
@@ -205,11 +224,10 @@
             for k in sides:
                 for column in range(0, lateral, LANES):
                     value = block(t, c, starts[k] + column, every).astype(jnp.bfloat16)
-                    (state_near, state_far)[k - PIECES][t + 1, here, column : column + LANES] = value
+                    state_side[t + 1, k - PIECES, here, column : column + LANES] = value
                 remote(t + 1, c, k).start()
 
     columns = range(0, width, LANES)
-    last = TICKS - 1
     for c in range(CHUNKS):
         here = rows_of(c)
         sideways(last, c)
@@ -222,16 +240,11 @@
         for column in columns:
             out[0, here, column : column + LANES] = block(last, c, column, rounds[-1]).astype(jnp.bfloat16)
 
-    @pl.loop(0, TICKS)
-    def _(t):
-        for c in range(CHUNKS):
-            for k in sides:
-                remote(t, c, k).wait_send()
-
-            @pl.when(has_next)
-            def _():
-                for k in every:
-                    remote(t, c, k).wait_send()
+    copy_to(near, state_side, got_side, 1, side_sem.at[0, 0]).wait_send()
+
+    @pl.when(has_next)
+    def _():
+        copy_to(targets[0], state_on, got_on, 0, on_sem.at[0]).wait_send()
 
 
 def on_device(count, traces, operator, loads, seeds, patches, trace_map):
@@ -242,9 +255,10 @@
     bf16, i32 = jnp.bfloat16, jnp.int32
     anywhere = pl.BlockSpec(memory_space=pl.ANY)
     dma = pltpu.SemaphoreType.DMA
-    flows = PIECES + 2
-    side = pltpu.VMEM((TICKS, rows, lateral), bf16)
-    slots = (pltpu.VMEM((TICKS, PIECES, rows, onward // PIECES), bf16), side, side)
+    slots = (
+        pltpu.VMEM((TICKS, PIECES, rows, onward // PIECES), bf16),
+        pltpu.VMEM((TICKS, 2, rows, lateral), bf16),
+    )
     return pl.pallas_call(
         functools.partial(kernel, count),
         name="sweep",
@@ -265,9 +279,10 @@
             pltpu.VMEM((TICKS, depth, rows), bf16),
             dma((4,)),
             dma((2,)),
-            dma((CHUNKS, flows)),
-            dma((TICKS, CHUNKS, flows)),
-            dma((TICKS, CHUNKS, flows)),
+            dma((CHUNKS, 2)),
+            dma((2,)),
+            dma((TICKS * CHUNKS + PIECES - 1,)),
+            dma((2, CHUNKS)),
         ],
         compiler_params=pltpu.CompilerParams(
             collective_id=0, has_side_effects=True, vmem_limit_bytes=60 * 2**20

time: 73 us -> 71.8 us (0.984)
  Pallas kernels: 71.9 us -> 70.7 us
    pallas_call x1, Pallas kernels: 71.9 us -> 70.7 us  [on_device(): pl.pallas_call(functools.partial(kernel, count), name='sweep', out_shape=...]
where the time goes in v1:
time: 71.8 us; the launch traced here: 71.7 us
  Pallas kernels  70.7 us (98%)
  local copies, waits for them, and re-layouts  0.97 us (1%)
    pallas_call x1, Pallas kernels, on_device(): pl.pallas_call(functools.partial(kernel, count), name='sweep', out_shape=...  70.7 us

profile of v1, /device:TPU:0, one launch (start us, length us, event | category | flops | bytes accessed | tf_op | source)
XLA Modules:
  0.0 71.7 jit_solution(9931290811911939222)
XLA Ops:
  0.0 70.7 %sweep.1 = bf16[1,256,2048]{2,1,0:T(8,128)(2,1)S(1)} custom-call(bf16[1,256,2048]{2,1,0:T(8,128)(2,1)} %traces.1, bf16[1,2048,2048]{2,1,0:T(8,128)(2,1)} %operator.1, bf16[1,16,2048]{2,1,0:T(8,128)(2,1)} %loads.1, s32[1,256]{1,0:T(1,128)} %bitcast.1, s32[1,256]{1,0:T(1,128)} %patches.1, s32[1,1024]{1,0:T(1,128)} %trace_map.1), custom_call_target="tpu_custom_call" | custom-call | tf_op jit(solution)/shard_map/sweep/pallas_call | solution.py:262
  70.7 1.0 %copy.8 = bf16[1,256,2048]{2,1,0:T(8,128)(2,1)} copy(bf16[1,256,2048]{2,1,0:T(8,128)(2,1)S(1)} %sweep.1) | data formatting | bytes 2097152

commit v2 on v1

v2 whole, which is shorter than its diff:
```python
import functools

import jax
import jax.numpy as jnp
from jax import lax
from jax.experimental import pallas as pl
from jax.experimental.pallas import tpu as pltpu
from jax.sharding import PartitionSpec as P

TICKS = 6
STRIPS = 4
CHUNKS = 2
PIECES = 4
ROUNDS = ((0, 1), (2,), (3,))
DEFER = 3
PERIOD = 97
LANES = 512
MESH = pl.DeviceIdType.MESH


def dot(a, b):
    return jnp.dot(a, b, preferred_element_type=jnp.float32)


def kernel(
    count, traces, operator, loads, seeds, patches, trace_map, early, total, mapped, tail,
    weights, one_hot, state_on, state_side, got_on, got_side,
    small, picked,
    in_sem, send_sem, on_sem, side_sem,
):
    me = lax.axis_index("bay")
    rows, size = state_on.shape[2:]
    lateral = state_side.shape[3]
    onward = PIECES * size
    width = onward + 2 * lateral
    depth = loads.shape[1]
    part = rows // CHUNKS
    has_next = me + STRIPS < count
    has_prev = me >= STRIPS
    near = me + 1 - 2 * (me % 2)
    far = me + 2 - 4 * ((me // 2) % 2)
    barrier = pltpu.get_barrier_semaphore()

    def greet(device):
        pl.semaphore_signal(barrier, inc=1, device_id={"bay": device}, device_id_type=MESH)

    @pl.when(has_prev)
    def _():
        greet(me - STRIPS)

    greet(far)
    greet(near)

    starts = tuple(q * size for q in range(PIECES)) + (onward, onward + lateral)
    sizes = (size,) * PIECES + (lateral, lateral)
    sides = (PIECES, PIECES + 1)

    def rows_of(c):
        return pl.ds(c * part, part)

    def span(pieces):
        return pl.ds(pieces[0], len(pieces))

    def held(t, c, k):
        if k < PIECES:
            return state_on.at[t, k, rows_of(c)]
        return state_side.at[t, k - PIECES, rows_of(c)]

    first = [
        pltpu.make_async_copy(
            traces.at[0, rows_of(c), pl.ds(starts[k], sizes[k])], held(0, c, k), in_sem.at[k // PIECES]
        )
        for c in range(CHUNKS)
        for k in range(PIECES + 2)
    ]
    lists = [
        pltpu.make_async_copy(src, small.at[:, pl.ds(begin, src.shape[1])], in_sem.at[2])
        for src, begin in ((trace_map, 0), (seeds, onward), (patches, onward + rows))
    ]
    upper = pltpu.make_async_copy(operator.at[0, pl.ds(0, onward)], weights.at[pl.ds(0, onward)], in_sem.at[0])
    lower = [
        pltpu.make_async_copy(operator.at[0, pl.ds(onward, onward)], weights.at[pl.ds(onward, onward)], in_sem.at[1]),
        pltpu.make_async_copy(loads.at[0], weights.at[pl.ds(width, depth)], in_sem.at[1]),
    ]
    for copy in first + lists:
        copy.start()

    pl.semaphore_wait(barrier, 2 + has_next.astype(jnp.int32))

    last = TICKS - 1

    def copy_to(device, src, dst, kind, signal):
        return pltpu.make_async_remote_copy(
            src_ref=src,
            dst_ref=dst,
            send_sem=send_sem.at[kind],
            recv_sem=signal,
            device_id={"bay": device},
            device_id_type=MESH,
        )

    def to_next(t, c, pieces):
        alone = 0
        if c == CHUNKS - 1 and pieces in ROUNDS:
            alone = ROUNDS.index(pieces) * ((t + 1) // TICKS)
        here = (t, span(pieces), rows_of(c))
        return copy_to(me + STRIPS, state_on.at[here], got_on.at[here], 0, on_sem.at[t * CHUNKS + c + alone])

    def to_side(t, c, k):
        here = (t, k - PIECES, rows_of(c))
        return copy_to((near, far)[k - PIECES], state_side.at[here], got_side.at[here], 1, side_sem.at[t % 2, c])

    def both_sides(t, c):
        here = (t, slice(None), rows_of(c))
        return copy_to(near, state_side.at[here], got_side.at[here], 1, side_sem.at[t % 2, c])

    def send_onward(t, c, groups):
        @pl.when(has_next)
        def _():
            for pieces in groups:
                to_next(t, c, pieces).start()

    def loaded(ref, which):
        pltpu.make_async_copy(ref, ref, in_sem.at[which]).wait()

    every = tuple(range(PIECES))
    deferred = jnp.logical_not(has_prev) & (me % 2 == 1)

    def send_first(c, when):
        @pl.when(has_next & when)
        def _():
            to_next(0, c, every).start()

    loaded(state_on.at[0], 0)
    send_first(0, True)
    for c in range(1, CHUNKS):
        send_first(c, jnp.logical_not(deferred))
    loaded(state_side.at[0], 1)
    for c in range(CHUNKS):
        for k in sides:
            to_side(0, c, k).start()
    for copy in [upper] + lower:
        copy.start()

    @pl.when(jnp.logical_not(has_prev))
    def _():
        got_on[...] = jnp.zeros_like(got_on)

    loaded(small, 2)
    map_row = small[:, :onward]
    seed_row = small[:, onward : onward + rows]
    pick_row = small[:, onward + rows :]
    place = lax.broadcasted_iota(jnp.int32, one_hot.shape, 0)
    one_hot[...] = jnp.where(place == map_row, 1.0, 0.0).astype(jnp.bfloat16)
    value = seed_row * 7
    guess = (value.astype(jnp.float32) * (1.0 / PERIOD)).astype(jnp.int32)
    rest = value - guess * PERIOD
    rest = jnp.where(rest < 0, rest + PERIOD, rest)
    rest = jnp.where(rest >= PERIOD, rest - PERIOD, rest)
    chosen = lax.broadcasted_iota(jnp.int32, picked.shape[1:], 0) == pick_row
    for t in range(TICKS):
        turn = rest + (13 * t) % PERIOD
        turn = jnp.where(turn >= PERIOD, turn - PERIOD, turn)
        amplitude = (turn - 48).astype(jnp.float32) / 32.0
        picked[t] = jnp.where(chosen, amplitude, 0.0).astype(jnp.bfloat16)

    upper.wait()

    @pl.loop(0, width // LANES)
    def _(n):
        at = pl.ds(pl.multiple_of(n * LANES, LANES), LANES)
        for m in range(0, onward, 256):
            mapped[m : m + 256, at] = dot(one_hot[m : m + 256, :], weights[:onward, at]).astype(jnp.bfloat16)

        for c in range(1, CHUNKS):
            send_first(c, deferred & (n == DEFER))

    loaded(weights.at[pl.ds(onward, onward + depth)], 1)

    def sideways(t, c):
        here = rows_of(c)
        both_sides(t, c).wait_recv()

        @pl.loop(0, width // LANES)
        def _(n):
            at = pl.ds(pl.multiple_of(n * LANES, LANES), LANES)
            source = lax.dot_general(
                picked[t, :, here], weights[width:, at], (((0,), (0,)), ((), ())), preferred_element_type=jnp.float32
            )
            total[here, at] = (
                source
                + dot(got_side[t, 0, here], weights[onward : onward + lateral, at])
                + dot(got_side[t, 1, here], weights[onward + lateral : width, at])
            )

    def arrive(t, c, pieces):
        @pl.when(has_prev)
        def _():
            to_next(t, c, pieces).wait_recv()

    def block(t, c, column, pieces):
        here = rows_of(c)
        at = pl.ds(column, LANES)
        incoming = jnp.concatenate([got_on[t, q, here] for q in pieces], axis=1)
        return total[here, at] + dot(incoming, mapped[pieces[0] * size : (pieces[-1] + 1) * size, at])

    @pl.loop(0, TICKS - 1)
    def _(t):
        for c in range(CHUNKS):
            here = rows_of(c)
            sideways(t, c)
            arrive(t, c, every)
            for column in range(0, onward, LANES):
                value = block(t, c, column, every).astype(jnp.bfloat16)
                pieces = tuple(range(column // size, (column + LANES) // size))
                for q in pieces:
                    state_on[t + 1, q, here] = value[:, q * size - column : (q + 1) * size - column]
                cut = c == CHUNKS - 1 and pieces not in ROUNDS
                send_onward(t + 1, c, [p for p in ROUNDS if p[0] in pieces] if cut else (pieces,))
            for k in sides:
                for column in range(0, lateral, LANES):
                    value = block(t, c, starts[k] + column, every).astype(jnp.bfloat16)
                    state_side[t + 1, k - PIECES, here, column : column + LANES] = value
                to_side(t + 1, c, k).start()

    columns = range(0, width, LANES)
    for c in range(CHUNKS - 1):
        sideways(last, c)
        arrive(last, c, every)
        for column in columns:
            early[rows_of(c), column : column + LANES] = block(last, c, column, every).astype(jnp.bfloat16)
    c = CHUNKS - 1
    here = rows_of(c)
    sideways(last, c)
    for pieces in ROUNDS[:-1]:
        arrive(last, c, pieces)
        for column in columns:
            total[here, column : column + LANES] = block(last, c, column, pieces)
    arrive(last, c, ROUNDS[-1])
    tail[...] = jnp.concatenate([got_on[last, q, here] for q in ROUNDS[-1]], axis=1)

    copy_to(near, state_side, got_side, 1, side_sem.at[0, 0]).wait_send()

    @pl.when(has_next)
    def _():
        copy_to(me + STRIPS, state_on, got_on, 0, on_sem.at[0]).wait_send()


def finish(early, total, mapped, tail, out, late, sem):
    done, width = early.shape
    depth = tail.shape[1]
    bulk = pltpu.make_async_copy(early, out.at[0, pl.ds(0, done)], sem.at[0])
    bulk.start()
    for column in range(0, width, LANES):
        at = pl.ds(column, LANES)
        late[:, at] = (total[done:, at] + dot(tail[...], mapped[mapped.shape[0] - depth :, at])).astype(jnp.bfloat16)
        pltpu.make_async_copy(late.at[:, at], out.at[0, pl.ds(done, late.shape[0]), at], sem.at[1]).start()
    bulk.wait()
    pltpu.make_async_copy(late, out.at[0, pl.ds(done, late.shape[0])], sem.at[1]).wait()


def on_device(count, traces, operator, loads, seeds, patches, trace_map):
    _, rows, width = traces.shape
    onward = trace_map.shape[1]
    lateral = (width - onward) // 2
    depth = loads.shape[1]
    bf16, i32 = jnp.bfloat16, jnp.int32
    anywhere = pl.BlockSpec(memory_space=pltpu.HBM)
    dma = pltpu.SemaphoreType.DMA
    slots = (
        pltpu.VMEM((TICKS, PIECES, rows, onward // PIECES), bf16),
        pltpu.VMEM((TICKS, 2, rows, lateral), bf16),
    )
    local = pl.BlockSpec(memory_space=pltpu.VMEM)
    part = rows // CHUNKS
    parts = pl.pallas_call(
        functools.partial(kernel, count),
        name="sweep",
        out_shape=(
            pltpu.VMEM((rows - part, width), bf16),
            pltpu.VMEM((rows, width), jnp.float32),
            pltpu.VMEM((onward, width), bf16),
            pltpu.VMEM((part, len(ROUNDS[-1]) * (onward // PIECES)), bf16),
        ),
        in_specs=[anywhere] * 6,
        out_specs=(local,) * 4,
        scratch_shapes=[
            pltpu.VMEM((width + depth, width), bf16),
            pltpu.VMEM((onward, onward), bf16),
            *slots,
            *slots,
            pltpu.VMEM((1, onward + 2 * rows), i32),
            pltpu.VMEM((TICKS, depth, rows), bf16),
            dma((3,)),
            dma((2,)),
            dma((TICKS * CHUNKS + len(ROUNDS) - 1,)),
            dma((2, CHUNKS)),
        ],
        compiler_params=pltpu.CompilerParams(
            collective_id=0, has_side_effects=True, vmem_limit_bytes=50 * 2**20
        ),
    )(traces, operator, loads, seeds.reshape(1, rows), patches, trace_map)
    return pl.pallas_call(
        finish,
        name="finish",
        out_shape=jax.ShapeDtypeStruct(traces.shape, bf16),
        in_specs=[local] * 4,
        out_specs=anywhere,
        scratch_shapes=[pltpu.VMEM((part, width), bf16), dma((2,))],
        compiler_params=pltpu.CompilerParams(vmem_limit_bytes=4 * 2**20),
    )(*parts)


def solution(mesh):
    placed = (
        P("bay", "groups", None),
        P("bay", None, None),
        P("bay", None, None),
        P("groups"),
        P("bay", "groups"),
        P("bay", None),
    )
    return jax.shard_map(
        functools.partial(on_device, mesh.shape["bay"]),
        mesh=mesh,
        in_specs=placed,
        out_specs=P("bay", "groups", None),
        check_vma=False,
    )
```

time: 71.8 us -> 71.4 us (level); the launches traced: 71.7 us -> 70.5 us
  local copies, waits for them, and re-layouts: 0.97 us -> 0 us
    pallas_call x1, Pallas kernels: 70.7 us -> 69.5 us  [on_device(): pl.pallas_call(functools.partial(kernel, count), name='sweep', out_shape=...]
    pallas_call x0 -> x1, Pallas kernels: none -> 1.02 us  [on_device(): pl.pallas_call(finish, name='finish', out_shape=jax.ShapeDtypeStruct(trac...]
    unnamed x1 -> x0, local copies, waits for them, and re-layouts: 0.97 us -> none
where the time goes in v2:
time: 71.4 us; the launch traced here: 70.5 us
  Pallas kernels  70.5 us (99%)
    pallas_call x1, Pallas kernels, on_device(): pl.pallas_call(functools.partial(kernel, count), name='sweep', out_shape=...  69.5 us

profile of v2, /device:TPU:0, one launch (start us, length us, event | category | flops | bytes accessed | tf_op | source)
XLA Modules:
  0.0 70.5 jit_solution(11102766050392682862)
XLA Ops:
  0.0 69.5 %sweep.1 = (bf16[128,2048]{1,0:T(8,128)(2,1)S(1)}, f32[256,2048]{1,0:T(8,128)S(1)}, bf16[1024,2048]{1,0:T(8,128)(2,1)S(1)}, bf16[128,256]{1,0:T(8,128)(2,1)S(1)}) custom-call(bf16[1,256,2048]{2,1,0:T(8,128)(2,1)} %traces.1, bf16[1,2048,2048]{2,1,0:T(8,128)(2,1)} %operator.1, bf16[1,16,2048]{2,1,0:T(8,128)(2,1)} %loads.1, s32[1,256]{1,0:T(1,128)} %bitcast.1, ...), custom_call_target="tpu_custom_call" | custom-call | tf_op jit(solution)/shard_map/sweep/pallas_call | solution.py:276
  69.5 1.0 %finish.1 = bf16[1,256,2048]{2,1,0:T(8,128)(2,1)} custom-call(bf16[128,2048]{1,0:T(8,128)(2,1)S(1)} %get-tuple-element.9.early, f32[256,2048]{1,0:T(8,128)S(1)} %get-tuple-element.10.total, bf16[1024,2048]{1,0:T(8,128)(2,1)S(1)} %get-tuple-element.11.mapped, bf16[128,256]{1,0:T(8,128)(2,1)S(1)} %get-tuple-element.12.tail), custom_call_target="tpu_custom_call" | custom-call | tf_op jit(solution)/shard_map/finish/pallas_call | solution.py:303

commit v3 on v2

--- a/solution.py
+++ b/solution.py
@@ -26,7 +26,54 @@
     count, traces, operator, loads, seeds, patches, trace_map, early, total, mapped, tail,
     weights, one_hot, state_on, state_side, got_on, got_side,
     small, picked,
-    in_sem, send_sem, on_sem, side_sem,
+    send_sem, end_sem,
+):
+    me = lax.axis_index("bay")
+    next_device = {"bay": me + STRIPS}
+    has_next = me + STRIPS < count
+    has_prev = me >= STRIPS
+    part = state_on.shape[2] // CHUNKS
+    final = (TICKS - 1, pl.ds(ROUNDS[-1][0], len(ROUNDS[-1])), pl.ds((CHUNKS - 1) * part, part))
+
+    def onward_copy(at, signal):
+        return pltpu.make_async_remote_copy(
+            src_ref=state_on.at[at],
+            dst_ref=got_on.at[at],
+            send_sem=send_sem.at[0],
+            recv_sem=signal,
+            device_id=next_device,
+            device_id_type=MESH,
+        )
+
+    dma = pltpu.SemaphoreType.DMA
+    pl.run_scoped(
+        functools.partial(
+            sweep, count, traces, operator, loads, seeds, patches, trace_map, early, total, mapped,
+            weights, one_hot, state_on, state_side, got_on, got_side, small, picked, send_sem, end_sem,
+        ),
+        dma((3,)),
+        dma((TICKS * CHUNKS + len(ROUNDS) - 2,)),
+        dma((2, CHUNKS)),
+    )
+
+    @pl.when(has_prev)
+    def _():
+        onward_copy(final, end_sem.at[0]).wait_recv()
+
+    at, pieces, here = final
+    tail[...] = jnp.concatenate([got_on[at, q, here] for q in ROUNDS[-1]], axis=1)
+    pltpu.make_async_copy(state_side, state_side, send_sem.at[1]).wait()
+
+    @pl.when(has_next)
+    def _():
+        pltpu.make_async_copy(state_on, state_on, send_sem.at[0]).wait()
+
+
+def sweep(
+    count, traces, operator, loads, seeds, patches, trace_map, early, total, mapped,
+    weights, one_hot, state_on, state_side, got_on, got_side,
+    small, picked, send_sem, end_sem,
+    in_sem, on_sem, side_sem,
 ):
     me = lax.axis_index("bay")
     rows, size = state_on.shape[2:]
@@ -100,11 +147,12 @@
         )
 
     def to_next(t, c, pieces):
-        alone = 0
-        if c == CHUNKS - 1 and pieces in ROUNDS:
-            alone = ROUNDS.index(pieces) * ((t + 1) // TICKS)
+        signal = on_sem.at[t * CHUNKS + c]
+        if isinstance(t, int) and t == last and c == CHUNKS - 1:
+            order = ROUNDS.index(pieces)
+            signal = end_sem.at[0] if order == len(ROUNDS) - 1 else on_sem.at[t * CHUNKS + c + order]
         here = (t, span(pieces), rows_of(c))
-        return copy_to(me + STRIPS, state_on.at[here], got_on.at[here], 0, on_sem.at[t * CHUNKS + c + alone])
+        return copy_to(me + STRIPS, state_on.at[here], got_on.at[here], 0, signal)
 
     def to_side(t, c, k):
         here = (t, k - PIECES, rows_of(c))
@@ -204,8 +252,7 @@
         incoming = jnp.concatenate([got_on[t, q, here] for q in pieces], axis=1)
         return total[here, at] + dot(incoming, mapped[pieces[0] * size : (pieces[-1] + 1) * size, at])
 
-    @pl.loop(0, TICKS - 1)
-    def _(t):
+    def tick(t):
         for c in range(CHUNKS):
             here = rows_of(c)
             sideways(t, c)
@@ -215,13 +262,16 @@
                 pieces = tuple(range(column // size, (column + LANES) // size))
                 for q in pieces:
                     state_on[t + 1, q, here] = value[:, q * size - column : (q + 1) * size - column]
-                cut = c == CHUNKS - 1 and pieces not in ROUNDS
+                cut = isinstance(t, int) and c == CHUNKS - 1
                 send_onward(t + 1, c, [p for p in ROUNDS if p[0] in pieces] if cut else (pieces,))
             for k in sides:
                 for column in range(0, lateral, LANES):
                     value = block(t, c, starts[k] + column, every).astype(jnp.bfloat16)
                     state_side[t + 1, k - PIECES, here, column : column + LANES] = value
                 to_side(t + 1, c, k).start()
+
+    pl.loop(0, TICKS - 2)(tick)
+    tick(TICKS - 2)
 
     columns = range(0, width, LANES)
     for c in range(CHUNKS - 1):
@@ -236,14 +286,6 @@
         arrive(last, c, pieces)
         for column in columns:
             total[here, column : column + LANES] = block(last, c, column, pieces)
-    arrive(last, c, ROUNDS[-1])
-    tail[...] = jnp.concatenate([got_on[last, q, here] for q in ROUNDS[-1]], axis=1)
-
-    copy_to(near, state_side, got_side, 1, side_sem.at[0, 0]).wait_send()
-
-    @pl.when(has_next)
-    def _():
-        copy_to(me + STRIPS, state_on, got_on, 0, on_sem.at[0]).wait_send()
 
 
 def finish(early, total, mapped, tail, out, late, sem):
@@ -291,10 +333,8 @@
             *slots,
             pltpu.VMEM((1, onward + 2 * rows), i32),
             pltpu.VMEM((TICKS, depth, rows), bf16),
-            dma((3,)),
             dma((2,)),
-            dma((TICKS * CHUNKS + len(ROUNDS) - 1,)),
-            dma((2, CHUNKS)),
+            dma((1,)),
         ],
         compiler_params=pltpu.CompilerParams(
             collective_id=0, has_side_effects=True, vmem_limit_bytes=50 * 2**20

time: 71.4 us -> 71.2 us (level)
  no operation moved by 1% of the time
where the time goes in v3:
time: 71.2 us; the launch traced here: 70.3 us
  Pallas kernels  70.3 us (99%)
    pallas_call x1, Pallas kernels, on_device(): pl.pallas_call(functools.partial(kernel, count), name='sweep', out_shape=...  69.3 us

profile of v3, /device:TPU:0, one launch (start us, length us, event | category | flops | bytes accessed | tf_op | source)
XLA Modules:
  0.0 70.3 jit_solution(14892313375250266460)
XLA Ops:
  0.0 69.3 %sweep.1 = (bf16[128,2048]{1,0:T(8,128)(2,1)S(1)}, f32[256,2048]{1,0:T(8,128)S(1)}, bf16[1024,2048]{1,0:T(8,128)(2,1)S(1)}, bf16[128,256]{1,0:T(8,128)(2,1)S(1)}) custom-call(bf16[1,256,2048]{2,1,0:T(8,128)(2,1)} %traces.1, bf16[1,2048,2048]{2,1,0:T(8,128)(2,1)} %operator.1, bf16[1,16,2048]{2,1,0:T(8,128)(2,1)} %loads.1, s32[1,256]{1,0:T(1,128)} %bitcast.1, ...), custom_call_target="tpu_custom_call" | custom-call | tf_op jit(solution)/shard_map/sweep/pallas_call | solution.py:318
  69.3 1.0 %finish.1 = bf16[1,256,2048]{2,1,0:T(8,128)(2,1)} custom-call(bf16[128,2048]{1,0:T(8,128)(2,1)S(1)} %get-tuple-element.9.early, f32[256,2048]{1,0:T(8,128)S(1)} %get-tuple-element.10.total, bf16[1024,2048]{1,0:T(8,128)(2,1)S(1)} %get-tuple-element.11.mapped, bf16[128,256]{1,0:T(8,128)(2,1)S(1)} %get-tuple-element.12.tail), custom_call_target="tpu_custom_call" | custom-call | tf_op jit(solution)/shard_map/finish/pallas_call | solution.py:343

commit v4 on v3

--- a/solution.py
+++ b/solution.py
@@ -39,7 +39,7 @@
         return pltpu.make_async_remote_copy(
             src_ref=state_on.at[at],
             dst_ref=got_on.at[at],
-            send_sem=send_sem.at[0],
+            send_sem=send_sem,
             recv_sem=signal,
             device_id=next_device,
             device_id_type=MESH,
@@ -54,26 +54,26 @@
         dma((3,)),
         dma((TICKS * CHUNKS + len(ROUNDS) - 2,)),
         dma((2, CHUNKS)),
+        dma(()),
     )
 
     @pl.when(has_prev)
     def _():
-        onward_copy(final, end_sem.at[0]).wait_recv()
+        onward_copy(final, end_sem).wait_recv()
 
     at, pieces, here = final
     tail[...] = jnp.concatenate([got_on[at, q, here] for q in ROUNDS[-1]], axis=1)
-    pltpu.make_async_copy(state_side, state_side, send_sem.at[1]).wait()
 
     @pl.when(has_next)
     def _():
-        pltpu.make_async_copy(state_on, state_on, send_sem.at[0]).wait()
+        pltpu.make_async_copy(state_on, state_on, send_sem).wait()
 
 
 def sweep(
     count, traces, operator, loads, seeds, patches, trace_map, early, total, mapped,
     weights, one_hot, state_on, state_side, got_on, got_side,
     small, picked, send_sem, end_sem,
-    in_sem, on_sem, side_sem,
+    in_sem, on_sem, side_sem, side_send,
 ):
     me = lax.axis_index("bay")
     rows, size = state_on.shape[2:]
@@ -140,7 +140,7 @@
         return pltpu.make_async_remote_copy(
             src_ref=src,
             dst_ref=dst,
-            send_sem=send_sem.at[kind],
+            send_sem=(send_sem, side_send)[kind],
             recv_sem=signal,
             device_id={"bay": device},
             device_id_type=MESH,
@@ -150,7 +150,7 @@
         signal = on_sem.at[t * CHUNKS + c]
         if isinstance(t, int) and t == last and c == CHUNKS - 1:
             order = ROUNDS.index(pieces)
-            signal = end_sem.at[0] if order == len(ROUNDS) - 1 else on_sem.at[t * CHUNKS + c + order]
+            signal = end_sem if order == len(ROUNDS) - 1 else on_sem.at[t * CHUNKS + c + order]
         here = (t, span(pieces), rows_of(c))
         return copy_to(me + STRIPS, state_on.at[here], got_on.at[here], 0, signal)
 
@@ -286,6 +286,7 @@
         arrive(last, c, pieces)
         for column in columns:
             total[here, column : column + LANES] = block(last, c, column, pieces)
+    pltpu.make_async_copy(state_side, state_side, side_send).wait()
 
 
 def finish(early, total, mapped, tail, out, late, sem):
@@ -333,8 +334,8 @@
             *slots,
             pltpu.VMEM((1, onward + 2 * rows), i32),
             pltpu.VMEM((TICKS, depth, rows), bf16),
-            dma((2,)),
-            dma((1,)),
+            dma(()),
+            dma(()),
         ],
         compiler_params=pltpu.CompilerParams(
             collective_id=0, has_side_effects=True, vmem_limit_bytes=50 * 2**20

time: 71.2 us -> 71.2 us (level)
  no operation moved by 1% of the time
where the time goes in v4:
time: 71.2 us; the launch traced here: 70.3 us
  Pallas kernels  70.3 us (99%)
    pallas_call x1, Pallas kernels, on_device(): pl.pallas_call(functools.partial(kernel, count), name='sweep', out_shape=...  69.3 us

profile of v4, /device:TPU:0, one launch (start us, length us, event | category | flops | bytes accessed | tf_op | source)
XLA Modules:
  0.0 70.3 jit_solution(7049054873962708620)
XLA Ops:
  0.0 69.3 %sweep.1 = (bf16[128,2048]{1,0:T(8,128)(2,1)S(1)}, f32[256,2048]{1,0:T(8,128)S(1)}, bf16[1024,2048]{1,0:T(8,128)(2,1)S(1)}, bf16[128,256]{1,0:T(8,128)(2,1)S(1)}) custom-call(bf16[1,256,2048]{2,1,0:T(8,128)(2,1)} %traces.1, bf16[1,2048,2048]{2,1,0:T(8,128)(2,1)} %operator.1, bf16[1,16,2048]{2,1,0:T(8,128)(2,1)} %loads.1, s32[1,256]{1,0:T(1,128)} %bitcast.1, ...), custom_call_target="tpu_custom_call" | custom-call | tf_op jit(solution)/shard_map/sweep/pallas_call | solution.py:319
  69.3 1.0 %finish.1 = bf16[1,256,2048]{2,1,0:T(8,128)(2,1)} custom-call(bf16[128,2048]{1,0:T(8,128)(2,1)S(1)} %get-tuple-element.9.early, f32[256,2048]{1,0:T(8,128)S(1)} %get-tuple-element.10.total, bf16[1024,2048]{1,0:T(8,128)(2,1)S(1)} %get-tuple-element.11.mapped, bf16[128,256]{1,0:T(8,128)(2,1)S(1)} %get-tuple-element.12.tail), custom_call_target="tpu_custom_call" | custom-call | tf_op jit(solution)/shard_map/finish/pallas_call | solution.py:344

commit v5 on v4

--- a/solution.py
+++ b/solution.py
@@ -187,9 +187,6 @@
     for c in range(CHUNKS):
         for k in sides:
             to_side(0, c, k).start()
-    for copy in [upper] + lower:
-        copy.start()
-
     @pl.when(jnp.logical_not(has_prev))
     def _():
         got_on[...] = jnp.zeros_like(got_on)
@@ -212,7 +209,10 @@
         amplitude = (turn - 48).astype(jnp.float32) / 32.0
         picked[t] = jnp.where(chosen, amplitude, 0.0).astype(jnp.bfloat16)
 
+    upper.start()
     upper.wait()
+    for copy in lower:
+        copy.start()
 
     @pl.loop(0, width // LANES)
     def _(n):
@@ -262,8 +262,10 @@
                 pieces = tuple(range(column // size, (column + LANES) // size))
                 for q in pieces:
                     state_on[t + 1, q, here] = value[:, q * size - column : (q + 1) * size - column]
-                cut = isinstance(t, int) and c == CHUNKS - 1
-                send_onward(t + 1, c, [p for p in ROUNDS if p[0] in pieces] if cut else (pieces,))
+                if isinstance(t, int) and c == CHUNKS - 1:
+                    send_onward(t + 1, c, [p for p in ROUNDS if p[0] in pieces])
+                elif pieces[-1] == PIECES - 1:
+                    send_onward(t + 1, c, (every,))
             for k in sides:
                 for column in range(0, lateral, LANES):
                     value = block(t, c, starts[k] + column, every).astype(jnp.bfloat16)

time: 71.2 us -> 71.2 us (level)
  no operation moved by 1% of the time
where the time goes in v5:
time: 71.2 us; the launch traced here: 70.7 us
  Pallas kernels  70.7 us (99%)
    pallas_call x1, Pallas kernels, on_device(): pl.pallas_call(functools.partial(kernel, count), name='sweep', out_shape=...  69.6 us

profile of v5, /device:TPU:0, one launch (start us, length us, event | category | flops | bytes accessed | tf_op | source)
XLA Modules:
  0.0 70.7 jit_solution(2921520306695265751)
XLA Ops:
  0.0 69.6 %sweep.1 = (bf16[128,2048]{1,0:T(8,128)(2,1)S(1)}, f32[256,2048]{1,0:T(8,128)S(1)}, bf16[1024,2048]{1,0:T(8,128)(2,1)S(1)}, bf16[128,256]{1,0:T(8,128)(2,1)S(1)}) custom-call(bf16[1,256,2048]{2,1,0:T(8,128)(2,1)} %traces.1, bf16[1,2048,2048]{2,1,0:T(8,128)(2,1)} %operator.1, bf16[1,16,2048]{2,1,0:T(8,128)(2,1)} %loads.1, s32[1,256]{1,0:T(1,128)} %bitcast.1, ...), custom_call_target="tpu_custom_call" | custom-call | tf_op jit(solution)/shard_map/sweep/pallas_call | solution.py:321
  69.7 1.0 %finish.1 = bf16[1,256,2048]{2,1,0:T(8,128)(2,1)} custom-call(bf16[128,2048]{1,0:T(8,128)(2,1)S(1)} %get-tuple-element.9.early, f32[256,2048]{1,0:T(8,128)S(1)} %get-tuple-element.10.total, bf16[1024,2048]{1,0:T(8,128)(2,1)S(1)} %get-tuple-element.11.mapped, bf16[128,256]{1,0:T(8,128)(2,1)S(1)} %get-tuple-element.12.tail), custom_call_target="tpu_custom_call" | custom-call | tf_op jit(solution)/shard_map/finish/pallas_call | solution.py:346
